TPU v7x, 128 devices: a whole 4x4x4 slice. The times are simulated.
128 devices in a mesh: seg: 32 (over y, z, core), grp: 4 (over x).
Axes of the slice: x: 4, y: 4, z: 4, core: 2. Of those that a mesh axis runs over, the one named last changes fastest.
Arguments:
- basis: float32 [8, 3072, 128], P(None, ('seg', 'grp')), may hold values from -6 to 6
- coords: float32 [3072, 3, 128], P(('seg', 'grp')), may hold values from 0 to 4
- areas: float32 [3072, 128], P(('seg', 'grp')), may hold values from 0.5 to 2
- p2m: bfloat16 [3072, 121, 128], P(('seg', 'grp')), may hold values from -0.5 to 0.5
- l2p: bfloat16 [3072, 128, 121], P(('seg', 'grp')), may hold values from -0.5 to 0.5
- m2l: bfloat16 [316, 121, 121], replicated, may hold values from -0.0390625 to 0.0390625
- counts: int32 [128], P(('seg', 'grp')), may hold values from 8 to 24
- near_list: int32 [3072, 27], P(('seg', 'grp')), may hold values from 0 to 287
- far_list: int32 [3072, 189], P(('seg', 'grp')), may hold values from 0 to 287
- far_offset: int32 [3072, 189], P(('seg', 'grp')), may hold values from 0 to 315
Outputs:
- new_vector: float32 [3072, 128], P(('seg', 'grp'))
- hessenberg: float32 [9], replicated
Inputs may be any that keep to these rules, and one draw needn't show every extreme that they name: `near_list`: window indices follow the rule of the steps; entries may name empty slots or leaves beyond the ends of the curve, which contribute nothing. A device's live leaves are its first counts slots.
All inputs are finite; a program needn't handle non-finite values.
Results may differ from a plain program's by a relative error of at most 0.0012.
Values sent between devices are 32-bit elements; how exact they have to be, the bound alone decides.
A program may use at most 64 MiB of HBM per device.

v0:
```python
import math
import jax
import jax.numpy as jnp
from jax import lax
from jax.sharding import Mesh
from jax.sharding import PartitionSpec as P

SEG = ("seg_0", "seg_1", "seg_2")
SEG_GRP = ("seg_0", "seg_1", "seg_2", "grp")
four_pi = 12.566370614359172
epsilon = 1e-06
highest = lax.Precision.HIGHEST


def from_everyone(value, axis):
    copies = jnp.broadcast_to(value, (lax.axis_size(axis), *value.shape))
    return lax.all_to_all(copies, axis, split_axis=0, concat_axis=0, tiled=True)


def in_order(pieces, dim):
    lengths = list(pieces.shape[1:])
    lengths[dim] *= pieces.shape[0]
    return jnp.moveaxis(pieces, 0, dim).reshape(lengths)


def gathered_copies(value, axis, dim):
    pieces = from_everyone(value, axis)
    return in_order(pieces, dim)


def in_one_piece(arrays, axis, dim, along):
    widths = [math.prod(a.shape[along:]) for a in arrays]
    both = jnp.concatenate(
        [a.reshape(*a.shape[:along], w) for a, w in zip(arrays, widths)], axis=along
    )
    whole = gathered_copies(both, axis, dim)
    pieces = jnp.split(whole, [sum(widths[:k]) for k in range(1, len(widths))], axis=along)
    return tuple(
        (b.reshape(*whole.shape[:along], *a.shape[along:]) for a, b in zip(arrays, pieces))
    )


def with_halo(cells, sides, width):
    for axis, dim in sides:
        count = lax.axis_size(axis)
        ends = count - 1
        head = lax.slice_in_dim(cells, 0, width, axis=dim)
        tail = lax.slice_in_dim(cells, cells.shape[dim] - width, cells.shape[dim], axis=dim)
        cells = jnp.concatenate(
            [
                lax.ppermute(tail, axis, [(i, (i + 1) % count) for i in range(ends)]),
                cells,
                lax.ppermute(head, axis, [((i + 1) % count, i) for i in range(ends)]),
            ],
            axis=dim,
        )
    return cells


def by_axis(value, axes):
    for axis in axes:
        value = lax.psum(value, axis)
    return value


def near_field(coords, wide_panels, near_list):
    leaf_count = coords.shape[0]
    panels = coords.shape[2]

    def near_step(running, column):
        source = jnp.take(wide_panels, column, axis=0)
        square = jnp.zeros((leaf_count, panels, panels), jnp.float32)
        for component in range(3):
            spread = coords[:, component, :, None] - source[:, component, None, :]
            square = square + spread * spread
        source_area = source[:, 3, None, :]
        kernel = source_area / (four_pi * jnp.sqrt(square + source_area))
        return (running + jnp.sum(kernel * source[:, 4, None, :], axis=2), None)

    result, _ = lax.scan(near_step, jnp.zeros((leaf_count, panels), jnp.float32), near_list.T)
    return result


def far_field(wide_poles, m2l, far_list, far_offset):
    offsets = m2l.shape[0]
    gathered = jnp.take(wide_poles, far_list, axis=0)
    offset_hot = (
        far_offset[:, :, None] == lax.broadcasted_iota(jnp.int32, (1, 1, offsets), 2)
    ).astype(jnp.float32)
    summed = jnp.einsum("tfo,tfk->tok", offset_hot, gathered, precision=highest)
    return jnp.einsum("tok,oik->ti", summed, m2l.astype(jnp.float32), precision=highest)


def on_device(basis, coords, areas, p2m, l2p, m2l, counts, near_list, far_list, far_offset):
    leaf_count, panels = areas.shape
    krylov = basis.shape[0]
    slots = lax.broadcasted_iota(jnp.int32, (leaf_count, 1), 0)
    live_mask = (slots < counts[0]).astype(jnp.float32)
    current = basis[krylov - 1] * live_mask
    rounded = current.astype(jnp.bfloat16)
    multipoles = jnp.einsum("lkp,lp->lk", p2m, rounded, preferred_element_type=jnp.float32)
    packed = jnp.concatenate([coords, areas[:, None, :], current[:, None, :]], axis=1)
    group_panels, group_poles = in_one_piece((packed, multipoles), "grp", 0, 1)
    wide_panels, wide_poles = (
        with_halo(group_panels, ((SEG, 0),), group_panels.shape[0]),
        with_halo(group_poles, ((SEG, 0),), group_panels.shape[0]),
    )
    nearby = near_field(coords, wide_panels, near_list)
    local = far_field(wide_poles, m2l, far_list, far_offset).astype(jnp.bfloat16)
    distant = jnp.einsum("lpk,lk->lp", l2p, local, preferred_element_type=jnp.float32)
    image = (0.5 * current + nearby + distant) * live_mask
    masked = basis * live_mask[None]
    products = jnp.einsum("jlp,lp->j", masked, image, precision=highest)
    live_panels = jnp.sum(live_mask) * panels
    gram = jnp.einsum("ilp,jlp->ij", masked, masked, precision=highest)
    summed, population, gram_sum, energy = (
        by_axis(products, SEG_GRP),
        by_axis(live_panels, SEG_GRP),
        by_axis(gram, SEG_GRP),
        by_axis(jnp.sum(image * image), SEG_GRP),
    )
    coefficients = summed / population
    residue = image - jnp.einsum("j,jlp->lp", coefficients, masked, precision=highest)
    curvature = jnp.dot(
        coefficients, jnp.dot(gram_sum, coefficients, precision=highest), precision=highest
    )
    squares = energy - 2.0 * jnp.dot(coefficients, summed, precision=highest) + curvature
    scale = jnp.sqrt(squares / population + epsilon)
    return (residue / scale, jnp.concatenate([coefficients, scale[None]]))


def solution(mesh):
    torus = Mesh(
        mesh.devices.reshape(4, 4, 2, mesh.shape["grp"]), ("seg_0", "seg_1", "seg_2", "grp")
    )
    in_specs = (
        P(None, SEG_GRP, None),
        P(SEG_GRP, None, None),
        P(SEG_GRP, None),
        P(SEG_GRP, None, None),
        P(SEG_GRP, None, None),
        P(),
        P(SEG_GRP),
        P(SEG_GRP, None),
        P(SEG_GRP, None),
        P(SEG_GRP, None),
    )
    out_specs = (P(SEG_GRP, None), P())
    return jax.shard_map(
        on_device, mesh=torus, in_specs=in_specs, out_specs=out_specs, check_vma=False
    )
```

profile of v0, /device:TPU:0, one launch (start us, length us, event | category | flops | bytes accessed | tf_op | source)
XLA Modules:
  0.0 194.8 jit_solution(17818676448152926383)
XLA Ops:
  1.4 0.8 fusion.37
  2.2 0.8 bitcast_multiply_fusion
  3.0 1.6 fusion.27
  4.6 0.8 copy_bitcast_fusion
  5.4 0.7 broadcast_in_dim.39
  6.1 4.4 %all-to-all-start = ((f32[4,24,761]{2,1,0:T(8,128)}), f32[4,24,761]{2,1,0:T(8,128)S(1)}, u32[]{:S(2)}, u32[]{:S(2)}) async-start(f32[4,24,761]{2,1,0:T(8,128)} %broadcast_in_dim.39), calls=%async_computation | async-start | bytes 589824 | tf_op jit(solution)/shard_map/all_to_all | solution.py:17
  11.1 6.5 %all-to-all-done = f32[4,24,761]{2,1,0:T(8,128)S(1)} async-done(((f32[4,24,761]{2,1,0:T(8,128)}), f32[4,24,761]{2,1,0:T(8,128)S(1)}, u32[]{:S(2)}, u32[]{:S(2)}) %all-to-all-start) | async-done | bytes 292256 | tf_op jit(solution)/shard_map/all_to_all | solution.py:17
  17.6 1.3 collective-permute-start.3
  18.9 3.0 %collective-permute-start.2 = (f32[96,121]{1,0:T(8,128)S(1)}, f32[96,121]{1,0:T(8,128)S(1)}, u32[]{:S(2)}, u32[]{:S(2)}) collective-permute-start(f32[96,121]{1,0:T(8,128)S(1)} %split.9), channel_id=1, source_target_pairs={{0,4},{4,8},{8,12},{12,16},{16,20},{20,24},{24,28},{28,32},{32,36}... | collective-permute-start | bytes 139400 | tf_op jit(solution)/shard_map/ppermute | solution.py:51
  21.9 0.7 fusion.38
  23.4 0.9 copy.19
  24.3 1.3 collective-permute-start.1
  25.6 4.8 %collective-permute-start = (f32[96,5,128]{0,2,1:T(8,128)}, f32[96,5,128]{0,2,1:T(8,128)}, u32[]{:S(2)}, u32[]{:S(2)}) collective-permute-start(f32[96,5,128]{0,2,1:T(8,128)} %bitcast.9), channel_id=1, source_target_pairs={{0,4},{4,8},{8,12},{12,16},{16,20},{20,24},{24,28},{28,32},{32,36}... | collective-permute-start | bytes 737288 | tf_op jit(solution)/shard_map/ppermute | solution.py:51
  30.4 7.4 %gather_fusion.1 = f32[4536,121]{1,0:T(8,128)S(1)} fusion(f32[288,121]{1,0:T(8,128)S(1)} %pad_maximum_fusion.1, s32[5120]{0:T(1024)S(1)} %pad_clamp_fusion.1), kind=kCustom, calls=%fused_computation.1 | custom fusion | bytes 4408992 | tf_op jit(solution)/shard_map/jit(_take)/gather | solution.py:86
  37.9 1.6 reshape.114
  39.5 10.6 %fusion.3 = f32[24,316,121]{2,1,0:T(8,128)S(1)} fusion(s32[24,189]{1,0:T(8,128)S(1)} %copy-done.4, f32[24,189,121]{2,1,0:T(8,128)} %reshape.114, pred[24,189]{1,0:T(8,128)(4,1)S(1)} %compare_and_fusion.1), kind=kOutput, calls=%fused_computation.17 | convolution fusion | flops 2083244160 | bytes 5888760 | tf_op jit(solution)/shard_map/tfo,tfk->tok/dot_general | solution.py:90
  50.1 16.4 %fusion.19 = bf16[24,121,1]{1,0,2:T(8,128)(2,1)S(1)} fusion(bf16[316,121,121]{2,0,1:T(8,128)(2,1)} %param.17, f32[24,316,121]{2,1,0:T(8,128)S(1)} %fusion.3), kind=kOutput, calls=%fused_computation.25 | convolution fusion | flops 1332450944 | bytes 12929576 | tf_op jit(solution)/shard_map/tok,oik->ti/dot_general | solution.py:91
  66.9 1.6 pad_maximum_fusion
  69.0 82.7 %while.11 = (s32[]{:T(128)}, f32[24,128]{1,0:T(8,128)S(1)}, s32[27,24]{1,0:T(8,128)S(1)}, f32[288,5,128]{2,1,0:T(8,128)S(1)}, f32[24,3,128]{2,0,1:T(8,128)S(1)}, /*index=5*/s32[]{:T(128)}, s32[]{:T(128)}) while((s32[]{:T(128)}, f32[24,128]{1,0:T(8,128)S(1)}, s32[27,24]{1,0:T(8,128)S(1)}, f32[288,5,128]{2,1,0:T(8,128)S(1)}, ...), condition=%wide.region_2.3_spmd.clone, body=%wide.region_0.2_spmd.clone.sunk | while | flops 5131483 | bytes 594551 | solution.py:80
  69.1 0.6 gather_fusion
  69.8 2.2 %multiply_reduce_fusion.4 = f32[24,128]{1,0:T(8,128)S(1)} fusion(f32[24,128]{1,0:T(8,128)S(1)} %bitcast.99, f32[24,128]{1,0:T(8,128)S(1)} %bitcast.100, f32[24,128]{1,0:T(8,128)S(1)} %get-tuple-element.137, f32[24,128]{1,0:T(8,128)S(1)} %bitcast.101, f32[24,128]{1,0:T(8,128)S(1)} %get-tuple-element.139, f32[24,128]{1,0:T(8,128)S(1)} %bitcast.102, ...), kind=kLoop, calls=%fused_computation.2.clone.1 | loop fusion | flops 5108736 | bytes 110592 | tf_op jit(solution)/shard_map/while/body/eval_jaxpr/reduce_sum | solution.py:78
  72.2 0.6 gather_fusion
  72.9 2.2 %multiply_reduce_fusion.4 = f32[24,128]{1,0:T(8,128)S(1)} fusion(f32[24,128]{1,0:T(8,128)S(1)} %bitcast.99, f32[24,128]{1,0:T(8,128)S(1)} %bitcast.100, f32[24,128]{1,0:T(8,128)S(1)} %get-tuple-element.137, f32[24,128]{1,0:T(8,128)S(1)} %bitcast.101, f32[24,128]{1,0:T(8,128)S(1)} %get-tuple-element.139, f32[24,128]{1,0:T(8,128)S(1)} %bitcast.102, ...), kind=kLoop, calls=%fused_computation.2.clone.1 | loop fusion | flops 5108736 | bytes 110592 | tf_op jit(solution)/shard_map/while/body/eval_jaxpr/reduce_sum | solution.py:78
  75.2 0.6 gather_fusion
  76.0 2.2 %multiply_reduce_fusion.4 = f32[24,128]{1,0:T(8,128)S(1)} fusion(f32[24,128]{1,0:T(8,128)S(1)} %bitcast.99, f32[24,128]{1,0:T(8,128)S(1)} %bitcast.100, f32[24,128]{1,0:T(8,128)S(1)} %get-tuple-element.137, f32[24,128]{1,0:T(8,128)S(1)} %bitcast.101, f32[24,128]{1,0:T(8,128)S(1)} %get-tuple-element.139, f32[24,128]{1,0:T(8,128)S(1)} %bitcast.102, ...), kind=kLoop, calls=%fused_computation.2.clone.1 | loop fusion | flops 5108736 | bytes 110592 | tf_op jit(solution)/shard_map/while/body/eval_jaxpr/reduce_sum | solution.py:78
  78.3 0.6 gather_fusion
  79.0 2.2 %multiply_reduce_fusion.4 = f32[24,128]{1,0:T(8,128)S(1)} fusion(f32[24,128]{1,0:T(8,128)S(1)} %bitcast.99, f32[24,128]{1,0:T(8,128)S(1)} %bitcast.100, f32[24,128]{1,0:T(8,128)S(1)} %get-tuple-element.137, f32[24,128]{1,0:T(8,128)S(1)} %bitcast.101, f32[24,128]{1,0:T(8,128)S(1)} %get-tuple-element.139, f32[24,128]{1,0:T(8,128)S(1)} %bitcast.102, ...), kind=kLoop, calls=%fused_computation.2.clone.1 | loop fusion | flops 5108736 | bytes 110592 | tf_op jit(solution)/shard_map/while/body/eval_jaxpr/reduce_sum | solution.py:78
  82.1 2.2 %multiply_reduce_fusion.4 = f32[24,128]{1,0:T(8,128)S(1)} fusion(f32[24,128]{1,0:T(8,128)S(1)} %bitcast.99, f32[24,128]{1,0:T(8,128)S(1)} %bitcast.100, f32[24,128]{1,0:T(8,128)S(1)} %get-tuple-element.137, f32[24,128]{1,0:T(8,128)S(1)} %bitcast.101, f32[24,128]{1,0:T(8,128)S(1)} %get-tuple-element.139, f32[24,128]{1,0:T(8,128)S(1)} %bitcast.102, ...), kind=kLoop, calls=%fused_computation.2.clone.1 | loop fusion | flops 5108736 | bytes 110592 | tf_op jit(solution)/shard_map/while/body/eval_jaxpr/reduce_sum | solution.py:78
  85.1 2.2 %multiply_reduce_fusion.4 = f32[24,128]{1,0:T(8,128)S(1)} fusion(f32[24,128]{1,0:T(8,128)S(1)} %bitcast.99, f32[24,128]{1,0:T(8,128)S(1)} %bitcast.100, f32[24,128]{1,0:T(8,128)S(1)} %get-tuple-element.137, f32[24,128]{1,0:T(8,128)S(1)} %bitcast.101, f32[24,128]{1,0:T(8,128)S(1)} %get-tuple-element.139, f32[24,128]{1,0:T(8,128)S(1)} %bitcast.102, ...), kind=kLoop, calls=%fused_computation.2.clone.1 | loop fusion | flops 5108736 | bytes 110592 | tf_op jit(solution)/shard_map/while/body/eval_jaxpr/reduce_sum | solution.py:78
  88.2 2.2 %multiply_reduce_fusion.4 = f32[24,128]{1,0:T(8,128)S(1)} fusion(f32[24,128]{1,0:T(8,128)S(1)} %bitcast.99, f32[24,128]{1,0:T(8,128)S(1)} %bitcast.100, f32[24,128]{1,0:T(8,128)S(1)} %get-tuple-element.137, f32[24,128]{1,0:T(8,128)S(1)} %bitcast.101, f32[24,128]{1,0:T(8,128)S(1)} %get-tuple-element.139, f32[24,128]{1,0:T(8,128)S(1)} %bitcast.102, ...), kind=kLoop, calls=%fused_computation.2.clone.1 | loop fusion | flops 5108736 | bytes 110592 | tf_op jit(solution)/shard_map/while/body/eval_jaxpr/reduce_sum | solution.py:78
  91.3 2.2 %multiply_reduce_fusion.4 = f32[24,128]{1,0:T(8,128)S(1)} fusion(f32[24,128]{1,0:T(8,128)S(1)} %bitcast.99, f32[24,128]{1,0:T(8,128)S(1)} %bitcast.100, f32[24,128]{1,0:T(8,128)S(1)} %get-tuple-element.137, f32[24,128]{1,0:T(8,128)S(1)} %bitcast.101, f32[24,128]{1,0:T(8,128)S(1)} %get-tuple-element.139, f32[24,128]{1,0:T(8,128)S(1)} %bitcast.102, ...), kind=kLoop, calls=%fused_computation.2.clone.1 | loop fusion | flops 5108736 | bytes 110592 | tf_op jit(solution)/shard_map/while/body/eval_jaxpr/reduce_sum | solution.py:78
  94.3 2.2 %multiply_reduce_fusion.4 = f32[24,128]{1,0:T(8,128)S(1)} fusion(f32[24,128]{1,0:T(8,128)S(1)} %bitcast.99, f32[24,128]{1,0:T(8,128)S(1)} %bitcast.100, f32[24,128]{1,0:T(8,128)S(1)} %get-tuple-element.137, f32[24,128]{1,0:T(8,128)S(1)} %bitcast.101, f32[24,128]{1,0:T(8,128)S(1)} %get-tuple-element.139, f32[24,128]{1,0:T(8,128)S(1)} %bitcast.102, ...), kind=kLoop, calls=%fused_computation.2.clone.1 | loop fusion | flops 5108736 | bytes 110592 | tf_op jit(solution)/shard_map/while/body/eval_jaxpr/reduce_sum | solution.py:78
  96.7 0.6 gather_fusion
  97.4 2.2 %multiply_reduce_fusion.4 = f32[24,128]{1,0:T(8,128)S(1)} fusion(f32[24,128]{1,0:T(8,128)S(1)} %bitcast.99, f32[24,128]{1,0:T(8,128)S(1)} %bitcast.100, f32[24,128]{1,0:T(8,128)S(1)} %get-tuple-element.137, f32[24,128]{1,0:T(8,128)S(1)} %bitcast.101, f32[24,128]{1,0:T(8,128)S(1)} %get-tuple-element.139, f32[24,128]{1,0:T(8,128)S(1)} %bitcast.102, ...), kind=kLoop, calls=%fused_computation.2.clone.1 | loop fusion | flops 5108736 | bytes 110592 | tf_op jit(solution)/shard_map/while/body/eval_jaxpr/reduce_sum | solution.py:78
  99.7 0.6 gather_fusion
  100.5 2.2 %multiply_reduce_fusion.4 = f32[24,128]{1,0:T(8,128)S(1)} fusion(f32[24,128]{1,0:T(8,128)S(1)} %bitcast.99, f32[24,128]{1,0:T(8,128)S(1)} %bitcast.100, f32[24,128]{1,0:T(8,128)S(1)} %get-tuple-element.137, f32[24,128]{1,0:T(8,128)S(1)} %bitcast.101, f32[24,128]{1,0:T(8,128)S(1)} %get-tuple-element.139, f32[24,128]{1,0:T(8,128)S(1)} %bitcast.102, ...), kind=kLoop, calls=%fused_computation.2.clone.1 | loop fusion | flops 5108736 | bytes 110592 | tf_op jit(solution)/shard_map/while/body/eval_jaxpr/reduce_sum | solution.py:78
  102.8 0.6 gather_fusion
  103.5 2.2 %multiply_reduce_fusion.4 = f32[24,128]{1,0:T(8,128)S(1)} fusion(f32[24,128]{1,0:T(8,128)S(1)} %bitcast.99, f32[24,128]{1,0:T(8,128)S(1)} %bitcast.100, f32[24,128]{1,0:T(8,128)S(1)} %get-tuple-element.137, f32[24,128]{1,0:T(8,128)S(1)} %bitcast.101, f32[24,128]{1,0:T(8,128)S(1)} %get-tuple-element.139, f32[24,128]{1,0:T(8,128)S(1)} %bitcast.102, ...), kind=kLoop, calls=%fused_computation.2.clone.1 | loop fusion | flops 5108736 | bytes 110592 | tf_op jit(solution)/shard_map/while/body/eval_jaxpr/reduce_sum | solution.py:78
  105.9 0.6 gather_fusion
  106.6 2.2 %multiply_reduce_fusion.4 = f32[24,128]{1,0:T(8,128)S(1)} fusion(f32[24,128]{1,0:T(8,128)S(1)} %bitcast.99, f32[24,128]{1,0:T(8,128)S(1)} %bitcast.100, f32[24,128]{1,0:T(8,128)S(1)} %get-tuple-element.137, f32[24,128]{1,0:T(8,128)S(1)} %bitcast.101, f32[24,128]{1,0:T(8,128)S(1)} %get-tuple-element.139, f32[24,128]{1,0:T(8,128)S(1)} %bitcast.102, ...), kind=kLoop, calls=%fused_computation.2.clone.1 | loop fusion | flops 5108736 | bytes 110592 | tf_op jit(solution)/shard_map/while/body/eval_jaxpr/reduce_sum | solution.py:78
  109.7 2.2 %multiply_reduce_fusion.4 = f32[24,128]{1,0:T(8,128)S(1)} fusion(f32[24,128]{1,0:T(8,128)S(1)} %bitcast.99, f32[24,128]{1,0:T(8,128)S(1)} %bitcast.100, f32[24,128]{1,0:T(8,128)S(1)} %get-tuple-element.137, f32[24,128]{1,0:T(8,128)S(1)} %bitcast.101, f32[24,128]{1,0:T(8,128)S(1)} %get-tuple-element.139, f32[24,128]{1,0:T(8,128)S(1)} %bitcast.102, ...), kind=kLoop, calls=%fused_computation.2.clone.1 | loop fusion | flops 5108736 | bytes 110592 | tf_op jit(solution)/shard_map/while/body/eval_jaxpr/reduce_sum | solution.py:78
  112.7 2.2 %multiply_reduce_fusion.4 = f32[24,128]{1,0:T(8,128)S(1)} fusion(f32[24,128]{1,0:T(8,128)S(1)} %bitcast.99, f32[24,128]{1,0:T(8,128)S(1)} %bitcast.100, f32[24,128]{1,0:T(8,128)S(1)} %get-tuple-element.137, f32[24,128]{1,0:T(8,128)S(1)} %bitcast.101, f32[24,128]{1,0:T(8,128)S(1)} %get-tuple-element.139, f32[24,128]{1,0:T(8,128)S(1)} %bitcast.102, ...), kind=kLoop, calls=%fused_computation.2.clone.1 | loop fusion | flops 5108736 | bytes 110592 | tf_op jit(solution)/shard_map/while/body/eval_jaxpr/reduce_sum | solution.py:78
  115.8 2.2 %multiply_reduce_fusion.4 = f32[24,128]{1,0:T(8,128)S(1)} fusion(f32[24,128]{1,0:T(8,128)S(1)} %bitcast.99, f32[24,128]{1,0:T(8,128)S(1)} %bitcast.100, f32[24,128]{1,0:T(8,128)S(1)} %get-tuple-element.137, f32[24,128]{1,0:T(8,128)S(1)} %bitcast.101, f32[24,128]{1,0:T(8,128)S(1)} %get-tuple-element.139, f32[24,128]{1,0:T(8,128)S(1)} %bitcast.102, ...), kind=kLoop, calls=%fused_computation.2.clone.1 | loop fusion | flops 5108736 | bytes 110592 | tf_op jit(solution)/shard_map/while/body/eval_jaxpr/reduce_sum | solution.py:78
  118.8 2.2 %multiply_reduce_fusion.4 = f32[24,128]{1,0:T(8,128)S(1)} fusion(f32[24,128]{1,0:T(8,128)S(1)} %bitcast.99, f32[24,128]{1,0:T(8,128)S(1)} %bitcast.100, f32[24,128]{1,0:T(8,128)S(1)} %get-tuple-element.137, f32[24,128]{1,0:T(8,128)S(1)} %bitcast.101, f32[24,128]{1,0:T(8,128)S(1)} %get-tuple-element.139, f32[24,128]{1,0:T(8,128)S(1)} %bitcast.102, ...), kind=kLoop, calls=%fused_computation.2.clone.1 | loop fusion | flops 5108736 | bytes 110592 | tf_op jit(solution)/shard_map/while/body/eval_jaxpr/reduce_sum | solution.py:78
  121.9 2.2 %multiply_reduce_fusion.4 = f32[24,128]{1,0:T(8,128)S(1)} fusion(f32[24,128]{1,0:T(8,128)S(1)} %bitcast.99, f32[24,128]{1,0:T(8,128)S(1)} %bitcast.100, f32[24,128]{1,0:T(8,128)S(1)} %get-tuple-element.137, f32[24,128]{1,0:T(8,128)S(1)} %bitcast.101, f32[24,128]{1,0:T(8,128)S(1)} %get-tuple-element.139, f32[24,128]{1,0:T(8,128)S(1)} %bitcast.102, ...), kind=kLoop, calls=%fused_computation.2.clone.1 | loop fusion | flops 5108736 | bytes 110592 | tf_op jit(solution)/shard_map/while/body/eval_jaxpr/reduce_sum | solution.py:78
  125.0 2.2 %multiply_reduce_fusion.4 = f32[24,128]{1,0:T(8,128)S(1)} fusion(f32[24,128]{1,0:T(8,128)S(1)} %bitcast.99, f32[24,128]{1,0:T(8,128)S(1)} %bitcast.100, f32[24,128]{1,0:T(8,128)S(1)} %get-tuple-element.137, f32[24,128]{1,0:T(8,128)S(1)} %bitcast.101, f32[24,128]{1,0:T(8,128)S(1)} %get-tuple-element.139, f32[24,128]{1,0:T(8,128)S(1)} %bitcast.102, ...), kind=kLoop, calls=%fused_computation.2.clone.1 | loop fusion | flops 5108736 | bytes 110592 | tf_op jit(solution)/shard_map/while/body/eval_jaxpr/reduce_sum | solution.py:78
  127.3 0.6 gather_fusion
  128.0 2.2 %multiply_reduce_fusion.4 = f32[24,128]{1,0:T(8,128)S(1)} fusion(f32[24,128]{1,0:T(8,128)S(1)} %bitcast.99, f32[24,128]{1,0:T(8,128)S(1)} %bitcast.100, f32[24,128]{1,0:T(8,128)S(1)} %get-tuple-element.137, f32[24,128]{1,0:T(8,128)S(1)} %bitcast.101, f32[24,128]{1,0:T(8,128)S(1)} %get-tuple-element.139, f32[24,128]{1,0:T(8,128)S(1)} %bitcast.102, ...), kind=kLoop, calls=%fused_computation.2.clone.1 | loop fusion | flops 5108736 | bytes 110592 | tf_op jit(solution)/shard_map/while/body/eval_jaxpr/reduce_sum | solution.py:78
  131.1 2.2 %multiply_reduce_fusion.4 = f32[24,128]{1,0:T(8,128)S(1)} fusion(f32[24,128]{1,0:T(8,128)S(1)} %bitcast.99, f32[24,128]{1,0:T(8,128)S(1)} %bitcast.100, f32[24,128]{1,0:T(8,128)S(1)} %get-tuple-element.137, f32[24,128]{1,0:T(8,128)S(1)} %bitcast.101, f32[24,128]{1,0:T(8,128)S(1)} %get-tuple-element.139, f32[24,128]{1,0:T(8,128)S(1)} %bitcast.102, ...), kind=kLoop, calls=%fused_computation.2.clone.1 | loop fusion | flops 5108736 | bytes 110592 | tf_op jit(solution)/shard_map/while/body/eval_jaxpr/reduce_sum | solution.py:78
  134.2 2.2 %multiply_reduce_fusion.4 = f32[24,128]{1,0:T(8,128)S(1)} fusion(f32[24,128]{1,0:T(8,128)S(1)} %bitcast.99, f32[24,128]{1,0:T(8,128)S(1)} %bitcast.100, f32[24,128]{1,0:T(8,128)S(1)} %get-tuple-element.137, f32[24,128]{1,0:T(8,128)S(1)} %bitcast.101, f32[24,128]{1,0:T(8,128)S(1)} %get-tuple-element.139, f32[24,128]{1,0:T(8,128)S(1)} %bitcast.102, ...), kind=kLoop, calls=%fused_computation.2.clone.1 | loop fusion | flops 5108736 | bytes 110592 | tf_op jit(solution)/shard_map/while/body/eval_jaxpr/reduce_sum | solution.py:78
  137.2 2.2 %multiply_reduce_fusion.4 = f32[24,128]{1,0:T(8,128)S(1)} fusion(f32[24,128]{1,0:T(8,128)S(1)} %bitcast.99, f32[24,128]{1,0:T(8,128)S(1)} %bitcast.100, f32[24,128]{1,0:T(8,128)S(1)} %get-tuple-element.137, f32[24,128]{1,0:T(8,128)S(1)} %bitcast.101, f32[24,128]{1,0:T(8,128)S(1)} %get-tuple-element.139, f32[24,128]{1,0:T(8,128)S(1)} %bitcast.102, ...), kind=kLoop, calls=%fused_computation.2.clone.1 | loop fusion | flops 5108736 | bytes 110592 | tf_op jit(solution)/shard_map/while/body/eval_jaxpr/reduce_sum | solution.py:78
  140.3 2.2 %multiply_reduce_fusion.4 = f32[24,128]{1,0:T(8,128)S(1)} fusion(f32[24,128]{1,0:T(8,128)S(1)} %bitcast.99, f32[24,128]{1,0:T(8,128)S(1)} %bitcast.100, f32[24,128]{1,0:T(8,128)S(1)} %get-tuple-element.137, f32[24,128]{1,0:T(8,128)S(1)} %bitcast.101, f32[24,128]{1,0:T(8,128)S(1)} %get-tuple-element.139, f32[24,128]{1,0:T(8,128)S(1)} %bitcast.102, ...), kind=kLoop, calls=%fused_computation.2.clone.1 | loop fusion | flops 5108736 | bytes 110592 | tf_op jit(solution)/shard_map/while/body/eval_jaxpr/reduce_sum | solution.py:78
  143.3 2.2 %multiply_reduce_fusion.4 = f32[24,128]{1,0:T(8,128)S(1)} fusion(f32[24,128]{1,0:T(8,128)S(1)} %bitcast.99, f32[24,128]{1,0:T(8,128)S(1)} %bitcast.100, f32[24,128]{1,0:T(8,128)S(1)} %get-tuple-element.137, f32[24,128]{1,0:T(8,128)S(1)} %bitcast.101, f32[24,128]{1,0:T(8,128)S(1)} %get-tuple-element.139, f32[24,128]{1,0:T(8,128)S(1)} %bitcast.102, ...), kind=kLoop, calls=%fused_computation.2.clone.1 | loop fusion | flops 5108736 | bytes 110592 | tf_op jit(solution)/shard_map/while/body/eval_jaxpr/reduce_sum | solution.py:78
  146.4 2.2 %multiply_reduce_fusion.4 = f32[24,128]{1,0:T(8,128)S(1)} fusion(f32[24,128]{1,0:T(8,128)S(1)} %bitcast.99, f32[24,128]{1,0:T(8,128)S(1)} %bitcast.100, f32[24,128]{1,0:T(8,128)S(1)} %get-tuple-element.137, f32[24,128]{1,0:T(8,128)S(1)} %bitcast.101, f32[24,128]{1,0:T(8,128)S(1)} %get-tuple-element.139, f32[24,128]{1,0:T(8,128)S(1)} %bitcast.102, ...), kind=kLoop, calls=%fused_computation.2.clone.1 | loop fusion | flops 5108736 | bytes 110592 | tf_op jit(solution)/shard_map/while/body/eval_jaxpr/reduce_sum | solution.py:78
  149.5 2.2 %multiply_reduce_fusion.4 = f32[24,128]{1,0:T(8,128)S(1)} fusion(f32[24,128]{1,0:T(8,128)S(1)} %bitcast.99, f32[24,128]{1,0:T(8,128)S(1)} %bitcast.100, f32[24,128]{1,0:T(8,128)S(1)} %get-tuple-element.137, f32[24,128]{1,0:T(8,128)S(1)} %bitcast.101, f32[24,128]{1,0:T(8,128)S(1)} %get-tuple-element.139, f32[24,128]{1,0:T(8,128)S(1)} %bitcast.102, ...), kind=kLoop, calls=%fused_computation.2.clone.1 | loop fusion | flops 5108736 | bytes 110592 | tf_op jit(solution)/shard_map/while/body/eval_jaxpr/reduce_sum | solution.py:78
  151.7 0.7 multiply_reduce_fusion.1
  152.7 14.8 %all-reduce.2 = (f32[8]{0:T(128)S(1)}, f32[]{:T(128)}, f32[]{:T(128)}, f32[8,8]{1,0:T(8,128)S(1)}) all-reduce(f32[8]{0:T(128)S(1)} %convolution_bitcast_fusion.2, f32[]{:T(128)S(6)} %mul.76, f32[]{:T(128)} %get-tuple-element.86, f32[8,8]{1,0:T(8,128)S(1)} %convolution_bitcast_fusion), channel_id=1, replica_groups=mesh['seg_0'=4,'seg_1'=4,'seg_2'=2,'grp'=4] {'seg_0'}, use_global_device_ids=true, to_apply=%region_3.4 | all-reduce | flops 74 | bytes 592 | tf_op jit(solution)/shard_map/psum | solution.py:62
  167.5 8.4 %all-reduce.1 = (f32[8]{0:T(128)S(1)}, f32[]{:T(128)}, f32[]{:T(128)}, f32[8,8]{1,0:T(8,128)S(1)}) all-reduce(f32[8]{0:T(128)S(1)} %get-tuple-element.76, f32[]{:T(128)} %get-tuple-element.77, f32[]{:T(128)} %get-tuple-element.78, f32[8,8]{1,0:T(8,128)S(1)} %get-tuple-element.79), channel_id=1, replica_groups=mesh['seg_0'=4,'seg_1'=4,'seg_2'=2,'grp'=4] {'seg_1'}, use_global_device_ids=true, to_apply=%region_4.5 | all-reduce | flops 74 | bytes 592 | tf_op jit(solution)/shard_map/psum | solution.py:62
  176.0 3.1 %all-reduce.3 = (f32[8]{0:T(128)S(1)}, f32[]{:T(128)}, f32[]{:T(128)}, f32[8,8]{1,0:T(8,128)S(1)}) all-reduce(f32[8]{0:T(128)S(1)} %get-tuple-element.72, f32[]{:T(128)} %get-tuple-element.73, f32[]{:T(128)} %get-tuple-element.74, f32[8,8]{1,0:T(8,128)S(1)} %get-tuple-element.75), channel_id=1, replica_groups=mesh['seg_0'=4,'seg_1'=4,'seg_2'=2,'grp'=4] {'seg_2'}, use_global_device_ids=true, to_apply=%region_5.6 | all-reduce | flops 74 | bytes 592 | tf_op jit(solution)/shard_map/psum | solution.py:62
  179.0 9.6 %all-reduce = (f32[8]{0:T(128)S(1)}, f32[]{:T(128)}, f32[]{:T(128)}, f32[8,8]{1,0:T(8,128)S(1)}) all-reduce(f32[8]{0:T(128)S(1)} %get-tuple-element.80, f32[]{:T(128)} %get-tuple-element.81, f32[]{:T(128)} %get-tuple-element.82, f32[8,8]{1,0:T(8,128)S(1)} %get-tuple-element.83), channel_id=1, replica_groups=mesh['seg_0'=4,'seg_1'=4,'seg_2'=2,'grp'=4] {'grp'}, use_global_device_ids=true, to_apply=%region_6.7 | all-reduce | flops 74 | bytes 592 | tf_op jit(solution)/shard_map/psum | solution.py:62
  188.7 1.3 multiply_reduce_fusion.2
  190.2 0.7 fusion.29
  193.6 0.6 pad_maximum_fusion.3
  194.2 0.6 subtract_divide_fusion
  (240 shorter events, 17.5 us)
Async XLA Ops:
  0.6 65.9 %copy-start = (bf16[24,128,121]{1,0,2:T(8,128)(2,1)S(1)}, bf16[24,128,121]{1,0,2:T(8,128)(2,1)}, u32[]{:S(2)}) copy-start(bf16[24,128,121]{1,0,2:T(8,128)(2,1)} %param.16) | copy-start | bytes 2230276
  0.6 9.9 %copy-start.2 = (f32[8,24,128]{2,1,0:T(8,128)S(1)}, f32[8,24,128]{2,1,0:T(8,128)}, u32[]{:S(2)}) copy-start(f32[8,24,128]{2,1,0:T(8,128)} %param.12) | copy-start | bytes 294916
  0.7 10.0 %copy-start.3 = (s32[24,189]{1,0:T(8,128)S(1)}, s32[24,189]{1,0:T(8,128)}, u32[]{:S(2)}) copy-start(s32[24,189]{1,0:T(8,128)} %param.20) | copy-start | bytes 54436
  0.7 21.9 %copy-start.5 = (s32[24,27]{1,0:T(8,128)S(1)}, s32[24,27]{1,0:T(8,128)}, u32[]{:S(2)}) copy-start(s32[24,27]{1,0:T(8,128)} %param.19) | copy-start | bytes 7780
  6.1 11.4 %all-to-all-start = ((f32[4,24,761]{2,1,0:T(8,128)}), f32[4,24,761]{2,1,0:T(8,128)S(1)}, u32[]{:S(2)}, u32[]{:S(2)}) async-start(f32[4,24,761]{2,1,0:T(8,128)} %broadcast_in_dim.39), calls=%async_computation | async-start | bytes 589824 | tf_op jit(solution)/shard_map/all_to_all | solution.py:17
  17.6 12.9 %collective-permute-start.3 = (f32[96,121]{1,0:T(8,128)S(1)}, f32[96,121]{1,0:T(8,128)S(1)}, u32[]{:S(2)}, u32[]{:S(2)}) collective-permute-start(f32[96,121]{1,0:T(8,128)S(1)} %split.9), channel_id=1, source_target_pairs={{4,0},{8,4},{12,8},{16,12},{20,16},{24,20},{28,24},{32,28},{36,32}... | collective-permute-start | bytes 139400 | tf_op jit(solution)/shard_map/ppermute | solution.py:53
  18.9 11.6 %collective-permute-start.2 = (f32[96,121]{1,0:T(8,128)S(1)}, f32[96,121]{1,0:T(8,128)S(1)}, u32[]{:S(2)}, u32[]{:S(2)}) collective-permute-start(f32[96,121]{1,0:T(8,128)S(1)} %split.9), channel_id=1, source_target_pairs={{0,4},{4,8},{8,12},{12,16},{16,20},{20,24},{24,28},{28,32},{32,36}... | collective-permute-start | bytes 139400 | tf_op jit(solution)/shard_map/ppermute | solution.py:51
  24.3 42.5 %collective-permute-start.1 = (f32[96,5,128]{0,2,1:T(8,128)}, f32[96,5,128]{0,2,1:T(8,128)}, u32[]{:S(2)}, u32[]{:S(2)}) collective-permute-start(f32[96,5,128]{0,2,1:T(8,128)} %bitcast.9), channel_id=1, source_target_pairs={{4,0},{8,4},{12,8},{16,12},{20,16},{24,20},{28,24},{32,28},{36,32}... | collective-permute-start | bytes 737288 | tf_op jit(solution)/shard_map/ppermute | solution.py:53
  25.6 41.3 %collective-permute-start = (f32[96,5,128]{0,2,1:T(8,128)}, f32[96,5,128]{0,2,1:T(8,128)}, u32[]{:S(2)}, u32[]{:S(2)}) collective-permute-start(f32[96,5,128]{0,2,1:T(8,128)} %bitcast.9), channel_id=1, source_target_pairs={{0,4},{4,8},{8,12},{12,16},{16,20},{20,24},{24,28},{28,32},{32,36}... | collective-permute-start | bytes 737288 | tf_op jit(solution)/shard_map/ppermute | solution.py:51
  37.9 1.6 copy-start.4
  66.8 2.2 %copy-start.1 = (f32[24,3,128]{2,0,1:T(8,128)S(1)}, f32[24,3,128]{2,0,1:T(8,128)}, u32[]{:S(2)}) copy-start(f32[24,3,128]{2,0,1:T(8,128)} %param.13) | copy-start | bytes 110596
where the time goes:
time: 195 us
  other arithmetic  71.5 us (37%)
  blocking collectives  36 us (18%)
  matrix products  30.5 us (16%)
  local copies, waits for them, and re-layouts  28.4 us (15%)
  starting transfers between devices  14.8 us (8%)
  waiting for transfers between devices  6.47 us (3%)
  between operations  4.89 us (3%)
  loops' own time  2.26 us (1%)
    reduce_sum x27, other arithmetic, near_step(): return (running + jnp.sum(kernel * source[:, 4, None, :], axis=2), None)  59.9 us
    psum x4, blocking collectives, by_axis(): value = lax.psum(value, axis)  36 us
    dot_general x1, matrix products, far_field(): jnp.einsum('tok,oik->ti', summed, m2l.astype(jnp.float32), precision=high...  16.4 us
    gather x27, local copies, waits for them, and re-layouts, near_step(): source = jnp.take(wide_panels, column, axis=0)  15.6 us
    dot_general x1, matrix products, far_field(): summed = jnp.einsum('tfo,tfk->tok', offset_hot, gathered, precision=highest)  10.6 us
    gather x2, local copies, waits for them, and re-layouts, far_field(): gathered = jnp.take(wide_poles, far_list, axis=0)  9 us
    ppermute x2, starting transfers between devices, with_halo(): lax.ppermute(tail, axis, [(i, (i + 1) % count) for i in range(ends)])  7.85 us
    all_to_all x1, waiting for transfers between devices, from_everyone(): return lax.all_to_all(copies, axis, split_axis=0, concat_axis=0, tiled=True)  6.46 us
  transfers between devices with their start and end apart: 5, of which 1 were waited for; matrix products, arithmetic and copies ran while one was open for 20% of the time, Pallas kernels for 0%

commit v1 on v0

--- a/solution.py
+++ b/solution.py
@@ -59,7 +59,7 @@
 
 def by_axis(value, axes):
     for axis in axes:
-        value = lax.psum(value, axis)
+        value = jnp.sum(lax.all_gather(value, axis), axis=0)
     return value
 
 

time: 195 us -> 248 us (1.27)
  blocking collectives: 36 us -> 73 us
  local copies, waits for them, and re-layouts: 28.4 us -> 42.8 us
  waiting for transfers between devices: 6.47 us -> 0.01 us
  other arithmetic: 71.5 us -> 76.2 us
  between operations: 4.89 us -> 7.55 us
    all_gather x0 -> x4, blocking collectives: none -> 40.5 us  [by_axis(): value = jnp.sum(lax.all_gather(value, axis), axis=0)]
    psum x4 -> x0, blocking collectives: 36 us -> none  [by_axis(): value = lax.psum(value, axis)]
    unnamed x0 -> x4, blocking collectives: none -> 32.5 us
    unnamed x14 -> x50, local copies, waits for them, and re-layouts: 0.66 us -> 14.7 us
    all_to_all x1, waiting for transfers between devices: 6.46 us -> 0.01 us  [from_everyone(): return lax.all_to_all(copies, axis, split_axis=0, concat_axis=0, tiled=True)]
    reduce_sum x0 -> x15, other arithmetic: none -> 4.89 us  [by_axis(): value = jnp.sum(lax.all_gather(value, axis), axis=0)]
  transfers between devices with their start and end apart: 5 -> 5, of which waited for: 1 -> 0; matrix products, arithmetic and copies ran while one was open for 20% -> 17% of each run, Pallas kernels for 0% -> 0%
where the time goes in v1:
time: 248 us; the launch traced here: 247 us
  other arithmetic  76.2 us (31%)
  blocking collectives  73 us (29%)
  local copies, waits for them, and re-layouts  42.8 us (17%)
  matrix products  30.5 us (12%)
  starting transfers between devices  14.5 us (6%)
  between operations  7.55 us (3%)
    reduce_sum x27, other arithmetic, near_step(): return (running + jnp.sum(kernel * source[:, 4, None, :], axis=2), None)  59.9 us
    all_gather x4, blocking collectives, by_axis(): value = jnp.sum(lax.all_gather(value, axis), axis=0)  40.5 us
    unnamed x4, blocking collectives  32.5 us
    dot_general x1, matrix products, far_field(): jnp.einsum('tok,oik->ti', summed, m2l.astype(jnp.float32), precision=high...  16.4 us
    gather x27, local copies, waits for them, and re-layouts, near_step(): source = jnp.take(wide_panels, column, axis=0)  15.6 us
    unnamed x50, local copies, waits for them, and re-layouts  14.7 us
    dot_general x1, matrix products, far_field(): summed = jnp.einsum('tfo,tfk->tok', offset_hot, gathered, precision=highest)  10.6 us
    gather x2, local copies, waits for them, and re-layouts, far_field(): gathered = jnp.take(wide_poles, far_list, axis=0)  9 us
  transfers between devices with their start and end apart: 5, of which 0 were waited for; matrix products, arithmetic and copies ran while one was open for 17% of the time, Pallas kernels for 0%

profile of v1, /device:TPU:0, one launch (start us, length us, event | category | flops | bytes accessed | tf_op | source)
XLA Modules:
  0.0 247.0 jit_solution(10930796046966705847)
XLA Ops:
  1.5 0.8 fusion.37
  2.3 0.8 bitcast_multiply_fusion
  3.0 1.6 fusion.27
  4.6 0.8 copy_bitcast_fusion
  5.5 0.7 broadcast_in_dim.39
  6.2 4.4 %all-to-all-start = ((f32[4,24,761]{2,1,0:T(8,128)}), f32[4,24,761]{2,1,0:T(8,128)S(1)}, u32[]{:S(2)}, u32[]{:S(2)}) async-start(f32[4,24,761]{2,1,0:T(8,128)} %broadcast_in_dim.39), calls=%async_computation | async-start | bytes 589824 | tf_op jit(solution)/shard_map/all_to_all | solution.py:17
  11.1 12.6 %all-gather.4 = f32[32,8]{1,0:T(8,128)S(1)} all-gather(f32[8,8]{1,0:T(8,128)S(1)} %convolution_bitcast_fusion), channel_id=6, replica_groups=mesh['seg_0'=4,'seg_1'=4,'seg_2'=2,'grp'=4] {'seg_0'}, dimensions={0}, use_global_device_ids=true | all-gather | bytes 1280 | tf_op jit(solution)/shard_map/all_gather | solution.py:62
  23.7 13.2 %all-gather.5 = f32[32,8]{1,0:T(8,128)S(1)} all-gather(f32[8,8]{1,0:T(8,128)S(1)} %bitcast_reduce_fusion.2), channel_id=7, replica_groups=mesh['seg_0'=4,'seg_1'=4,'seg_2'=2,'grp'=4] {'seg_1'}, dimensions={0}, use_global_device_ids=true | all-gather | bytes 1280 | tf_op jit(solution)/shard_map/all_gather | solution.py:62
  36.9 1.8 all-gather.6
  38.7 12.9 %all-gather.7 = f32[32,8]{1,0:T(8,128)S(1)} all-gather(f32[8,8]{1,0:T(8,128)S(1)} %bitcast_reduce_fusion.3), channel_id=9, replica_groups=mesh['seg_0'=4,'seg_1'=4,'seg_2'=2,'grp'=4] {'grp'}, dimensions={0}, use_global_device_ids=true | all-gather | bytes 1280 | tf_op jit(solution)/shard_map/all_gather | solution.py:62
  51.6 1.3 collective-permute-start.3
  52.9 3.0 %collective-permute-start.2 = (f32[96,121]{1,0:T(8,128)S(1)}, f32[96,121]{1,0:T(8,128)S(1)}, u32[]{:S(2)}, u32[]{:S(2)}) collective-permute-start(f32[96,121]{1,0:T(8,128)S(1)} %split.9), channel_id=1, source_target_pairs={{0,4},{4,8},{8,12},{12,16},{16,20},{20,24},{24,28},{28,32},{32,36}... | collective-permute-start | bytes 139400 | tf_op jit(solution)/shard_map/ppermute | solution.py:51
  56.0 0.7 fusion.38
  62.5 0.8 dynamic-update-slice.4
  63.4 0.9 copy.43
  64.3 1.3 collective-permute-start.1
  65.5 4.5 %collective-permute-start = (f32[96,5,128]{0,2,1:T(8,128)}, f32[96,5,128]{0,2,1:T(8,128)}, u32[]{:S(2)}, u32[]{:S(2)}) collective-permute-start(f32[96,5,128]{0,2,1:T(8,128)} %bitcast.9), channel_id=1, source_target_pairs={{0,4},{4,8},{8,12},{12,16},{16,20},{20,24},{24,28},{28,32},{32,36}... | collective-permute-start | bytes 737288 | tf_op jit(solution)/shard_map/ppermute | solution.py:51
  70.1 7.4 %gather_fusion.1 = f32[4536,121]{1,0:T(8,128)S(1)} fusion(f32[288,121]{1,0:T(8,128)S(1)} %pad_maximum_fusion.1, s32[5120]{0:T(1024)S(1)} %pad_clamp_fusion.1), kind=kCustom, calls=%fused_computation.1 | custom fusion | bytes 4408992 | tf_op jit(solution)/shard_map/jit(_take)/gather | solution.py:86
  77.5 1.6 reshape.114
  79.1 10.6 %fusion.3 = f32[24,316,121]{2,1,0:T(8,128)S(1)} fusion(s32[24,189]{1,0:T(8,128)S(1)} %copy-done.4, f32[24,189,121]{2,1,0:T(8,128)} %reshape.114, pred[24,189]{1,0:T(8,128)(4,1)S(1)} %compare_and_fusion.1), kind=kOutput, calls=%fused_computation.17 | convolution fusion | flops 2083244160 | bytes 5888760 | tf_op jit(solution)/shard_map/tfo,tfk->tok/dot_general | solution.py:90
  89.8 16.4 %fusion.19 = bf16[24,121,1]{1,0,2:T(8,128)(2,1)S(1)} fusion(bf16[316,121,121]{2,0,1:T(8,128)(2,1)} %param.17, f32[24,316,121]{2,1,0:T(8,128)S(1)} %fusion.3), kind=kOutput, calls=%fused_computation.25 | convolution fusion | flops 1332450944 | bytes 12929576 | tf_op jit(solution)/shard_map/tok,oik->ti/dot_general | solution.py:91
  106.5 1.6 pad_maximum_fusion
  108.7 82.7 %while.11 = (s32[]{:T(128)}, f32[24,128]{1,0:T(8,128)S(1)}, s32[27,24]{1,0:T(8,128)S(1)}, f32[288,5,128]{2,1,0:T(8,128)S(1)}, f32[24,3,128]{2,0,1:T(8,128)S(1)}, /*index=5*/s32[]{:T(128)}, s32[]{:T(128)}) while((s32[]{:T(128)}, f32[24,128]{1,0:T(8,128)S(1)}, s32[27,24]{1,0:T(8,128)S(1)}, f32[288,5,128]{2,1,0:T(8,128)S(1)}, ...), condition=%wide.region_2.3_spmd.clone, body=%wide.region_0.2_spmd.clone.sunk | while | flops 5131483 | bytes 594551 | solution.py:80
  109.5 2.2 multiply_reduce_fusion.4
  112.6 2.2 multiply_reduce_fusion.4
  115.6 2.2 multiply_reduce_fusion.4
  118.7 2.2 multiply_reduce_fusion.4
  121.7 2.2 multiply_reduce_fusion.4
  124.8 2.2 multiply_reduce_fusion.4
  127.9 2.2 multiply_reduce_fusion.4
  130.9 2.2 multiply_reduce_fusion.4
  134.0 2.2 multiply_reduce_fusion.4
  137.1 2.2 multiply_reduce_fusion.4
  140.1 2.2 multiply_reduce_fusion.4
  143.2 2.2 multiply_reduce_fusion.4
  146.3 2.2 multiply_reduce_fusion.4
  149.3 2.2 multiply_reduce_fusion.4
  152.4 2.2 multiply_reduce_fusion.4
  155.4 2.2 multiply_reduce_fusion.4
  158.5 2.2 multiply_reduce_fusion.4
  161.6 2.2 multiply_reduce_fusion.4
  164.6 2.2 multiply_reduce_fusion.4
  167.7 2.2 multiply_reduce_fusion.4
  170.8 2.2 multiply_reduce_fusion.4
  173.8 2.2 multiply_reduce_fusion.4
  176.9 2.2 multiply_reduce_fusion.4
  179.9 2.2 multiply_reduce_fusion.4
  183.0 2.2 multiply_reduce_fusion.4
  186.1 2.2 multiply_reduce_fusion.4
  189.1 2.2 multiply_reduce_fusion.4
  191.4 0.7 multiply_reduce_fusion.1
  192.3 1.6 dynamic-update-slice.8
  194.2 11.6 %all-reduce.14 = (f32[32]{0:T(128)S(1)}, f32[4]{0:T(128)S(1)}, f32[4]{0:T(128)S(1)}) all-reduce(f32[32]{0:T(128)S(1)} %dynamic-update-slice, f32[4]{0:T(128)S(1)} %dynamic-update-slice.4, f32[4]{0:T(128)S(1)} %dynamic-update-slice.8), channel_id=2, replica_groups=mesh['seg_0'=4,'seg_1'=4,'seg_2'=2,'grp'=4] {'seg_0'}, use_global_device_ids=true, to_apply=%add | all-reduce | flops 40 | bytes 320
  207.1 1.3 dynamic-update-slice.9
  208.4 1.3 dynamic-update-slice.5
  210.0 8.4 %all-reduce.13 = (f32[32]{0:T(128)S(1)}, f32[4]{0:T(128)S(1)}, f32[4]{0:T(128)S(1)}) all-reduce(f32[32]{0:T(128)S(1)} %dynamic-update-slice.1, f32[4]{0:T(128)S(1)} %dynamic-update-slice.5, f32[4]{0:T(128)S(1)} %dynamic-update-slice.9), channel_id=3, replica_groups=mesh['seg_0'=4,'seg_1'=4,'seg_2'=2,'grp'=4] {'seg_1'}, use_global_device_ids=true, to_apply=%add.1 | all-reduce | flops 40 | bytes 320
  219.7 1.4 dynamic-update-slice.10
  221.1 1.4 dynamic-update-slice.6
  222.7 2.4 all-reduce.15
  226.4 1.4 dynamic-update-slice.11
  227.8 1.4 dynamic-update-slice.7
  229.5 10.1 %all-reduce.12 = (f32[32]{0:T(128)S(1)}, f32[4]{0:T(128)S(1)}, f32[4]{0:T(128)S(1)}) all-reduce(f32[32]{0:T(128)S(1)} %dynamic-update-slice.3, f32[4]{0:T(128)S(1)} %dynamic-update-slice.7, f32[4]{0:T(128)S(1)} %dynamic-update-slice.11), channel_id=5, replica_groups=mesh['seg_0'=4,'seg_1'=4,'seg_2'=2,'grp'=4] {'grp'}, use_global_device_ids=true, to_apply=%add.3 | all-reduce | flops 40 | bytes 320
  240.2 1.2 multiply_reduce_fusion.2
  241.7 0.8 fusion.29
  (300 shorter events, 32.5 us)
Async XLA Ops:
  0.6 105.6 %copy-start = (bf16[24,128,121]{1,0,2:T(8,128)(2,1)S(1)}, bf16[24,128,121]{1,0,2:T(8,128)(2,1)}, u32[]{:S(2)}) copy-start(bf16[24,128,121]{1,0,2:T(8,128)(2,1)} %param.16) | copy-start | bytes 2230276
  0.6 56.1 %copy-start.9 = (u32[128]{0:T(128)S(1)}, u32[128]{0:T(128)}, u32[]{:S(2)}) copy-start(u32[128]{0:T(128)} %constant.80) | copy-start | bytes 1540
  0.7 56.7 %copy-start.8 = (u32[128]{0:T(128)S(1)}, u32[128]{0:T(128)}, u32[]{:S(2)}) copy-start(u32[128]{0:T(128)} %constant.75) | copy-start | bytes 1540
  0.7 58.5 %copy-start.7 = (u32[128]{0:T(128)S(1)}, u32[128]{0:T(128)}, u32[]{:S(2)}) copy-start(u32[128]{0:T(128)} %constant.70) | copy-start | bytes 1540
  0.7 59.7 %copy-start.6 = (u32[128]{0:T(128)S(1)}, u32[128]{0:T(128)}, u32[]{:S(2)}) copy-start(u32[128]{0:T(128)} %constant.65) | copy-start | bytes 1540
  0.7 9.9 %copy-start.2 = (f32[8,24,128]{2,1,0:T(8,128)S(1)}, f32[8,24,128]{2,1,0:T(8,128)}, u32[]{:S(2)}) copy-start(f32[8,24,128]{2,1,0:T(8,128)} %param.12) | copy-start | bytes 294916
  0.7 10.0 %copy-start.3 = (s32[24,189]{1,0:T(8,128)S(1)}, s32[24,189]{1,0:T(8,128)}, u32[]{:S(2)}) copy-start(s32[24,189]{1,0:T(8,128)} %param.20) | copy-start | bytes 54436
  0.7 61.0 %copy-start.5 = (s32[24,27]{1,0:T(8,128)S(1)}, s32[24,27]{1,0:T(8,128)}, u32[]{:S(2)}) copy-start(s32[24,27]{1,0:T(8,128)} %param.19) | copy-start | bytes 7780
  6.2 45.4 %all-to-all-start = ((f32[4,24,761]{2,1,0:T(8,128)}), f32[4,24,761]{2,1,0:T(8,128)S(1)}, u32[]{:S(2)}, u32[]{:S(2)}) async-start(f32[4,24,761]{2,1,0:T(8,128)} %broadcast_in_dim.39), calls=%async_computation | async-start | bytes 589824 | tf_op jit(solution)/shard_map/all_to_all | solution.py:17
  51.6 18.4 %collective-permute-start.3 = (f32[96,121]{1,0:T(8,128)S(1)}, f32[96,121]{1,0:T(8,128)S(1)}, u32[]{:S(2)}, u32[]{:S(2)}) collective-permute-start(f32[96,121]{1,0:T(8,128)S(1)} %split.9), channel_id=1, source_target_pairs={{4,0},{8,4},{12,8},{16,12},{20,16},{24,20},{28,24},{32,28},{36,32}... | collective-permute-start | bytes 139400 | tf_op jit(solution)/shard_map/ppermute | solution.py:53
  52.9 17.1 %collective-permute-start.2 = (f32[96,121]{1,0:T(8,128)S(1)}, f32[96,121]{1,0:T(8,128)S(1)}, u32[]{:S(2)}, u32[]{:S(2)}) collective-permute-start(f32[96,121]{1,0:T(8,128)S(1)} %split.9), channel_id=1, source_target_pairs={{0,4},{4,8},{8,12},{12,16},{16,20},{20,24},{24,28},{28,32},{32,36}... | collective-permute-start | bytes 139400 | tf_op jit(solution)/shard_map/ppermute | solution.py:51
  64.3 42.3 %collective-permute-start.1 = (f32[96,5,128]{0,2,1:T(8,128)}, f32[96,5,128]{0,2,1:T(8,128)}, u32[]{:S(2)}, u32[]{:S(2)}) collective-permute-start(f32[96,5,128]{0,2,1:T(8,128)} %bitcast.9), channel_id=1, source_target_pairs={{4,0},{8,4},{12,8},{16,12},{20,16},{24,20},{28,24},{32,28},{36,32}... | collective-permute-start | bytes 737288 | tf_op jit(solution)/shard_map/ppermute | solution.py:53
  65.5 41.0 %collective-permute-start = (f32[96,5,128]{0,2,1:T(8,128)}, f32[96,5,128]{0,2,1:T(8,128)}, u32[]{:S(2)}, u32[]{:S(2)}) collective-permute-start(f32[96,5,128]{0,2,1:T(8,128)} %bitcast.9), channel_id=1, source_target_pairs={{0,4},{4,8},{8,12},{12,16},{16,20},{20,24},{24,28},{28,32},{32,36}... | collective-permute-start | bytes 737288 | tf_op jit(solution)/shard_map/ppermute | solution.py:51
  77.5 1.6 copy-start.4
  106.5 2.2 copy-start.1
